TPU v7x, 32 devices: a whole 2x2x4 slice. The times are simulated.
32 devices in a mesh: bank: 8 (over y, x, core), lane: 4 (over z).
Axes of the slice: x: 2, y: 2, z: 4, core: 2. Of those that a mesh axis runs over, the one named last changes fastest.
Arguments:
- amplitudes: float32 [2, 128, 128, 128], P(None, ('bank', 'lane')), may hold values from -6 to 6
- energies: float32 [128, 128, 128], P(('bank', 'lane')), may hold values from -2 to 2
- phase_angles: float32 [2, 128], replicated, may hold values from 0.3 to 1.2
- mix_angles: float32 [2, 4], replicated, may hold values from 0.3 to 1.2
Outputs:
- final_parts: float32 [2, 128, 128, 128], P(None, ('bank', 'lane'))
- marginal: float32 [16, 128, 128], P('lane', 'bank')
All inputs are finite; a program needn't handle non-finite values.
Results may differ from a plain program's by a relative error of at most 0.0003.
Values sent between devices are 32-bit elements; how exact they have to be, the bound alone decides.
A program may use at most 64 MiB of HBM per device.

v0:
```python
import functools

import jax
import jax.numpy as jnp
from jax import lax
from jax.experimental import pallas as pl
from jax.experimental.pallas import tpu as pltpu
from jax.sharding import PartitionSpec as P

MESH = pl.DeviceIdType.MESH
SIN = (1.0, -1 / 6, 1 / 120, -1 / 5040, 1 / 362880, -1 / 39916800, 1 / 6227020800, -1 / 1307674368000)
COS = (1.0, -1 / 2, 1 / 24, -1 / 720, 1 / 40320, -1 / 3628800, 1 / 479001600, -1 / 87178291200, 1 / 20922789888000)


def series(square, terms):
    total = jnp.full_like(square, terms[-1])
    for term in terms[-2::-1]:
        total = total * square + term
    return total


def sin_cos(turn):
    square = turn * turn
    return turn * series(square, SIN), series(square, COS)


def split(x):
    high = x.astype(jnp.bfloat16)
    return high, (x - high.astype(jnp.float32)).astype(jnp.bfloat16)


def dot3(a, b):
    def one(x, y):
        return lax.dot_general(x, y, (((1,), (0,)), ((), ())), preferred_element_type=jnp.float32)

    return one(a[0], b[0]) + (one(a[1], b[0]) + one(a[0], b[1]))


def turn_table(count, cosine, sine):
    row = lax.broadcasted_iota(jnp.int32, (count, count), 0)
    col = lax.broadcasted_iota(jnp.int32, (count, count), 1)
    apart = row ^ col
    size = jnp.ones((count, count), jnp.float32)
    ones = jnp.zeros((count, count), jnp.int32)
    for place in range(count.bit_length() - 1):
        bit = (apart >> place) & 1
        size = size * jnp.where(bit == 1, sine, cosine)
        ones = ones + bit
    phase = ones & 3
    real = jnp.where(phase == 0, size, jnp.where(phase == 2, -size, 0.0))
    imag = jnp.where(phase == 1, -size, jnp.where(phase == 3, size, 0.0))
    return real, imag


def butterfly(re, im, stride, cosine, sine):
    count, rest = re.shape[0], re.shape[1:]
    parts = (count // (2 * stride), 2, stride) + rest
    re, im = re.reshape(parts), im.reshape(parts)
    ur, vr, ui, vi = re[:, 0], re[:, 1], im[:, 0], im[:, 1]
    new_re = jnp.stack([cosine * ur + sine * vi, cosine * vr + sine * ui], axis=1)
    new_im = jnp.stack([cosine * ui - sine * vr, cosine * vi - sine * ur], axis=1)
    return new_re.reshape((count,) + rest), new_im.reshape((count,) + rest)


def kernel(
    nb, nl, halves, amp_hbm, en_hbm, ph, mix, out, marg,
    amp, en, tmp, s_a, e_b, b_b, o_b, r_a, cs_b, sn_b, part_done, ch, m_in, load, send, recv,
):
    n = nb * nl
    depth, rows, lanes = amp.shape[1:]
    per = en.shape[1]
    step = per // halves
    tiled = per % 8 == 0
    units = rows // per
    piece = rows // nb
    last = 2 * halves + 1
    bank, lane = lax.axis_index("bank"), lax.axis_index("lane")
    me = bank * nl + lane

    load_en = pltpu.make_async_copy(en_hbm, en, load.at[0])
    load_amp = pltpu.make_async_copy(amp_hbm, amp, load.at[1])
    load_en.start()
    load_amp.start()
    barrier = pltpu.get_barrier_semaphore()

    def partner(k):
        return lax.rem(bank + nb - lax.rem(k, nb), nb), lax.rem(lane + k // nb, nl)

    def greet(k, carry):
        pl.semaphore_signal(barrier, 1, device_id=partner(k), device_id_type=MESH)
        return carry

    lax.fori_loop(1, n, greet, 0)

    def exchange(src, dst, which):
        def one(k, carry):
            to_bank, to_lane = partner(k)
            pltpu.make_async_remote_copy(
                src_ref=src.at[to_bank * nl + to_lane],
                dst_ref=dst.at[me],
                send_sem=send.at[which],
                recv_sem=recv.at[which],
                device_id=(to_bank, to_lane),
                device_id_type=MESH,
            ).start()
            return carry

        lax.fori_loop(1, n, one, 0)
        dst[me] = src[me]

    def arrived(dst, count, sems, which):
        most = dst.at[pl.ds(0, count - 1)]
        pltpu.make_async_copy(most, most, sems.at[which]).wait()

    cosines, sines = jnp.cos(mix[...]), jnp.sin(mix[...])

    def angle(layer, group):
        return cosines[layer : layer + 1, group : group + 1], sines[layer : layer + 1, group : group + 1]

    def tables(layer, count):
        real, imag = turn_table(lanes, *angle(layer, 0))
        by_lane = split(jnp.concatenate([jnp.concatenate([real, imag], 1), jnp.concatenate([-imag, real], 1)], 0))
        real, imag = turn_table(count, *angle(layer, 1))
        by_row = split(jnp.concatenate([jnp.concatenate([real, -imag], 1), jnp.concatenate([imag, real], 1)], 0))
        return by_lane, by_row

    def local_mix(layer, by_lane, by_row, count, read, write):
        pairs = [read(d) for d in range(depth)]
        stride = 1
        cosine, sine = (jnp.broadcast_to(x, (8, lanes))[None] for x in angle(layer, 2))
        re = jnp.stack([p[0] for p in pairs]).reshape(depth, count // 8, 8, lanes)
        im = jnp.stack([p[1] for p in pairs]).reshape(depth, count // 8, 8, lanes)
        while stride < depth:
            re, im = butterfly(re, im, stride, cosine, sine)
            stride *= 2
        re, im = re.reshape(depth, count, lanes), im.reshape(depth, count, lanes)
        for d in range(depth):
            both = dot3(split(jnp.concatenate([re[d], im[d]], 1)), by_lane)
            both = dot3(by_row, split(jnp.concatenate([both[:, :lanes], both[:, lanes:]], 0)))
            write(d, both[:count], both[count:])

    first_tables = tables(0, rows)
    second_tables = tables(1, rows // halves)

    load_en.wait()
    pl.semaphore_wait(barrier, n - 1)
    exchange(en, e_b, 0)
    load_amp.wait()

    def first(d):
        if tiled:
            e = en[pl.ds(d * units, units)].reshape(rows, lanes)
        else:
            e = tmp[0, d]
        sine, cosine = sin_cos(ph[0:1] * e)
        return amp[0, d] * cosine + amp[1, d] * sine, amp[1, d] * cosine - amp[0, d] * sine

    def to_units(d, re, im):
        if tiled:
            for part, x in enumerate((re, im)):
                x = x.reshape(units, halves, step, lanes)
                for h in range(halves):
                    s_a[h, pl.ds(d * units, units), part] = x[:, h]
        else:
            tmp[0, d] = re
            tmp[1, d] = im

    if not tiled:
        for d in range(depth):

            def spread(u, carry):
                tmp[0, d, pl.ds(u * per, per)] = en[d * units + u]
                return carry

            lax.fori_loop(0, units, spread, 0)
    local_mix(0, *first_tables, rows, first, to_units)
    if not tiled:
        for d in range(depth):

            def gather(u, carry):
                for part in range(2):
                    s_a[0, d * units + u, part] = tmp[part, d, pl.ds(u * per, per)]
                return carry

            lax.fori_loop(0, units, gather, 0)

    for h in range(halves):
        exchange(s_a.at[h], b_b.at[h], 1 + h)
    arrived(e_b, n, recv, 0)
    sine, cosine = sin_cos(ph[1:2][None] * e_b[...])
    sn_b[...] = sine
    cs_b[...] = cosine

    for h in range(halves):
        arrived(b_b.at[h], n, recv, 1 + h)
        span = pl.ds(h * step, step)
        re, im = b_b[h, :, 0], b_b[h, :, 1]
        for layer in range(2):
            stride = 1
            while stride < n:
                cosine, sine = (
                    jnp.broadcast_to(x, (step, lanes))[None, None] for x in angle(layer, 3 if stride < nl else 2)
                )
                re, im = butterfly(re, im, stride, cosine, sine)
                stride *= 2
            if layer == 0:
                cosine, sine = cs_b[:, span], sn_b[:, span]
                re, im = re * cosine + im * sine, im * cosine - re * sine
        o_b[h, :, 0] = re
        o_b[h, :, 1] = im
        exchange(o_b.at[h], r_a.at[h], 1 + halves + h)

    def second(h, d):
        if tiled:
            return tuple(
                r_a[h, pl.ds(d * units, units), part].reshape(rows // halves, lanes) for part in range(2)
            )
        return tmp[0, d], tmp[1, d]

    def keep(d, re, im):
        part_done[0, d] = re
        part_done[1, d] = im

    def pass_on(d):
        def one(k, carry):
            to_bank = lax.rem(bank + k, nb)
            pltpu.make_async_remote_copy(
                src_ref=ch.at[d, to_bank],
                dst_ref=m_in.at[bank, d],
                send_sem=send.at[last],
                recv_sem=recv.at[last],
                device_id=(to_bank, lane),
                device_id_type=MESH,
            ).start()
            return carry

        lax.fori_loop(1, nb, one, 0)
        m_in[bank, d] = ch[d, bank]

    def finish(d, re, im):
        if halves == 2:
            cosine, sine = angle(1, 1)
            ur, ui, vr, vi = part_done[0, d], part_done[1, d], re, im
            shape = (units, 1, step, lanes)
            re = [cosine * ur + sine * vi, cosine * vr + sine * ui]
            im = [cosine * ui - sine * vr, cosine * vi - sine * ur]
            re = jnp.concatenate([x.reshape(shape) for x in re], 1).reshape(rows, lanes)
            im = jnp.concatenate([x.reshape(shape) for x in im], 1).reshape(rows, lanes)
        chance = re * re + im * im
        for g in range(nb):
            ch[d, g] = chance[g * piece : (g + 1) * piece]
        out[0, d] = re
        out[1, d] = im
        pass_on(d)

    for h in range(halves):
        arrived(r_a.at[h], n, recv, 1 + halves + h)
        if not tiled:
            for d in range(depth):

                def place(u, carry):
                    for part in range(2):
                        tmp[part, d, pl.ds(u * per, per)] = r_a[h, d * units + u, part]
                    return carry

                lax.fori_loop(0, units, place, 0)
        write = finish if h == halves - 1 else keep
        local_mix(1, *second_tables, rows // halves, functools.partial(second, h), write)

    arrived(m_in, nb, recv, last)
    total = m_in[0]
    for g in range(1, nb):
        total = total + m_in[g]
    marg[...] = total * (1.0 / nb)
    arrived(e_b, n, send, 0)
    for h in range(halves):
        arrived(b_b.at[h], n, send, 1 + h)
        arrived(r_a.at[h], n, send, 1 + halves + h)
    arrived(m_in, nb, send, last)


def on_device(nb, nl, amplitudes, energies, phase_angles, mix_angles):
    _, depth, rows, lanes = amplitudes.shape
    n = nb * nl
    per = depth * rows // n
    halves = 2 if per % 16 == 0 else 1
    piece = rows // nb
    f32 = jnp.float32
    state = pltpu.VMEM((halves, n, 2, per // halves, lanes), f32)
    level = pltpu.VMEM((n, per, lanes), f32)
    vmem = pl.BlockSpec(memory_space=pltpu.VMEM)
    anywhere = pl.BlockSpec(memory_space=pl.ANY)
    whole = pltpu.VMEM((2, depth, rows, lanes), f32)
    return pl.pallas_call(
        functools.partial(kernel, nb, nl, halves),
        name="register",
        out_shape=(pltpu.VMEM(amplitudes.shape, f32), pltpu.VMEM((depth, piece, lanes), f32)),
        in_specs=[anywhere, anywhere, vmem, vmem],
        out_specs=(vmem, vmem),
        scratch_shapes=[
            whole,
            level,
            whole if per % 8 else pltpu.VMEM((1, 1, 8, 128), f32),
            state,
            level,
            state,
            state,
            state,
            level,
            level,
            pltpu.VMEM((2, depth, rows // halves, lanes), f32),
            pltpu.VMEM((depth, nb, piece, lanes), f32),
            pltpu.VMEM((nb, depth, piece, lanes), f32),
            pltpu.SemaphoreType.DMA((2,)),
            pltpu.SemaphoreType.DMA((2 * halves + 2,)),
            pltpu.SemaphoreType.DMA((2 * halves + 2,)),
        ],
        compiler_params=pltpu.CompilerParams(collective_id=0, has_side_effects=True),
    )(amplitudes, energies.reshape(n, per, lanes), phase_angles, mix_angles)


def solution(mesh):
    placed = (P(None, ("bank", "lane"), None, None), P(("bank", "lane"), None, None), P(), P())
    return jax.shard_map(
        functools.partial(on_device, mesh.shape["bank"], mesh.shape["lane"]),
        mesh=mesh,
        in_specs=placed,
        out_specs=(P(None, ("bank", "lane"), None, None), P("lane", "bank", None)),
        check_vma=False,
    )
```

profile of v0, /device:TPU:9, one launch (start us, length us, event | category | flops | bytes accessed | tf_op | source)
XLA Modules:
  0.0 42.8 jit_solution(639378012425648927)
XLA Ops:
  0.6 40.8 %register.1 = (f32[2,4,128,128]{3,2,1,0:T(8,128)S(1)}, f32[4,16,128]{2,1,0:T(8,128)S(1)}) custom-call(f32[2,4,128,128]{3,2,1,0:T(8,128)} %amp_hbm.1, f32[32,16,128]{2,1,0:T(8,128)} %bitcast.1, f32[2,128]{1,0:T(2,128)} %ph.1, f32[2,4]{1,0:T(2,128)} %mix.1), custom_call_target="tpu_custom_call" | custom-call | tf_op jit(solution)/shard_map/register/pallas_call | solution.py:294
  41.4 0.8 %copy.8 = f32[2,4,128,128]{3,2,1,0:T(8,128)} copy(f32[2,4,128,128]{3,2,1,0:T(8,128)S(1)} %get-tuple-element.2) | data formatting | bytes 1048576
  42.2 0.6 %copy.9 = f32[4,16,128]{2,1,0:T(8,128)} copy(f32[4,16,128]{2,1,0:T(8,128)S(1)} %get-tuple-element.3) | data formatting | bytes 65536
where the time goes:
time: 43.6 us; the launch traced here: 42.8 us
  Pallas kernels  40.8 us (94%)
  local copies, waits for them, and re-layouts  1.41 us (3%)
  between operations  0.64 us (1%)
    pallas_call x1, Pallas kernels, on_device(): pl.pallas_call(functools.partial(kernel, nb, nl, halves), name='register'...  40.8 us
    unnamed x2, local copies, waits for them, and re-layouts  1.41 us

commit v1 on v0

--- a/solution.py
+++ b/solution.py
@@ -63,34 +63,55 @@
 
 
 def kernel(
-    nb, nl, halves, amp_hbm, en_hbm, ph, mix, out, marg,
-    amp, en, tmp, s_a, e_b, b_b, o_b, r_a, cs_b, sn_b, part_done, ch, m_in, load, send, recv,
+    nb, nl, halves, amp_hbm, en_hbm, ph_hbm, mix_hbm, out, marg,
+    ph, mix, amp, en, e_l, tmp, s_a, e_b, b_b, o_b, r_a, cs_b, sn_b, part_done, ch, m_in, load, send, recv, line_in, lines_in, all_in,
 ):
     n = nb * nl
     depth, rows, lanes = amp.shape[1:]
-    per = en.shape[1]
+    per = en.shape[2]
     step = per // halves
     tiled = per % 8 == 0
     units = rows // per
     piece = rows // nb
-    last = 2 * halves + 1
+    last = 2 * halves + 2
+    hub = nl // 2 - 1
     bank, lane = lax.axis_index("bank"), lax.axis_index("lane")
     me = bank * nl + lane
 
     load_en = pltpu.make_async_copy(en_hbm, en, load.at[0])
     load_amp = pltpu.make_async_copy(amp_hbm, amp, load.at[1])
-    load_en.start()
-    load_amp.start()
+    load_ph = pltpu.make_async_copy(ph_hbm, ph, load.at[2])
+    load_mix = pltpu.make_async_copy(mix_hbm, mix, load.at[3])
     barrier = pltpu.get_barrier_semaphore()
 
     def partner(k):
         return lax.rem(bank + nb - lax.rem(k, nb), nb), lax.rem(lane + k // nb, nl)
 
-    def greet(k, carry):
-        pl.semaphore_signal(barrier, 1, device_id=partner(k), device_id_type=MESH)
+    def greet_line(k, carry):
+        to = lax.rem(lane + k, nl)
+
+        @pl.when(to != hub)
+        def _():
+            pl.semaphore_signal(barrier, 1, device_id=(bank, to), device_id_type=MESH)
+
         return carry
 
-    lax.fori_loop(1, n, greet, 0)
+    def signal_hubs(sem):
+        def one(k, carry):
+            pl.semaphore_signal(sem, 1, device_id=(lax.rem(bank + k, nb), hub), device_id_type=MESH)
+            return carry
+
+        lax.fori_loop(1, nb, one, 0)
+
+    @pl.when(lane == hub)
+    def _():
+        signal_hubs(barrier)
+
+    lax.fori_loop(1, nl, greet_line, 0)
+    load_en.start()
+    load_mix.start()
+    load_amp.start()
+    load_ph.start()
 
     def exchange(src, dst, which):
         def one(k, carry):
@@ -112,6 +133,33 @@
         most = dst.at[pl.ds(0, count - 1)]
         pltpu.make_async_copy(most, most, sems.at[which]).wait()
 
+    load_en.wait()
+    pl.semaphore_wait(barrier, jnp.where(lane == hub, nb - 1, nl - 1))
+
+    @pl.when(lane == hub + 1)
+    def _():
+        pl.semaphore_signal(line_in, 1, device_id=(bank, hub), device_id_type=MESH)
+
+    @pl.when(lane == hub)
+    def _():
+        pl.semaphore_wait(line_in, 1)
+        signal_hubs(lines_in)
+
+    def along_line(k, carry):
+        to = lax.rem(lane + k, nl)
+        pltpu.make_async_remote_copy(
+            src_ref=en.at[:, to],
+            dst_ref=e_l.at[lane],
+            send_sem=send.at[0],
+            recv_sem=recv.at[0],
+            device_id=(bank, to),
+            device_id_type=MESH,
+        ).start()
+        return carry
+
+    lax.fori_loop(1, nl, along_line, 0)
+    e_l[lane] = en[:, lane]
+    load_mix.wait()
     cosines, sines = jnp.cos(mix[...]), jnp.sin(mix[...])
 
     def angle(layer, group):
@@ -142,14 +190,12 @@
     first_tables = tables(0, rows)
     second_tables = tables(1, rows // halves)
 
-    load_en.wait()
-    pl.semaphore_wait(barrier, n - 1)
-    exchange(en, e_b, 0)
     load_amp.wait()
+    load_ph.wait()
 
     def first(d):
         if tiled:
-            e = en[pl.ds(d * units, units)].reshape(rows, lanes)
+            e = en[pl.ds(d * units // nl, units // nl)].reshape(rows, lanes)
         else:
             e = tmp[0, d]
         sine, cosine = sin_cos(ph[0:1] * e)
@@ -169,7 +215,7 @@
         for d in range(depth):
 
             def spread(u, carry):
-                tmp[0, d, pl.ds(u * per, per)] = en[d * units + u]
+                tmp[0, d, pl.ds(u * per, per)] = en[(d * units + u) // nl, lax.rem(d * units + u, nl)]
                 return carry
 
             lax.fori_loop(0, units, spread, 0)
@@ -184,10 +230,41 @@
 
             lax.fori_loop(0, units, gather, 0)
 
-    for h in range(halves):
+    @pl.when(lane == hub)
+    def _():
+        pl.semaphore_wait(lines_in, nb - 1)
+
+        def tell(k, carry):
+            pl.semaphore_signal(all_in, 1, device_id=(bank, lax.rem(lane + k, nl)), device_id_type=MESH)
+            return carry
+
+        lax.fori_loop(1, nl, tell, 0)
+
+    @pl.when(lane != hub)
+    def _():
+        pl.semaphore_wait(all_in, 1)
+
+    exchange(s_a.at[0], b_b.at[0], 1)
+    arrived(e_l, nl, recv, 0)
+
+    def across(k, carry):
+        to = lax.rem(bank + k, nb)
+        pltpu.make_async_remote_copy(
+            src_ref=e_l.at[:, to],
+            dst_ref=e_b.at[bank],
+            send_sem=send.at[last - 1],
+            recv_sem=recv.at[last - 1],
+            device_id=(to, lane),
+            device_id_type=MESH,
+        ).start()
+        return carry
+
+    lax.fori_loop(1, nb, across, 0)
+    e_b[bank] = e_l[:, bank]
+    for h in range(1, halves):
         exchange(s_a.at[h], b_b.at[h], 1 + h)
-    arrived(e_b, n, recv, 0)
-    sine, cosine = sin_cos(ph[1:2][None] * e_b[...])
+    arrived(e_b, nb, recv, last - 1)
+    sine, cosine = sin_cos(ph[1:2][None] * e_b[...].reshape(n, per, lanes))
     sn_b[...] = sine
     cs_b[...] = cosine
 
@@ -272,7 +349,8 @@
     for g in range(1, nb):
         total = total + m_in[g]
     marg[...] = total * (1.0 / nb)
-    arrived(e_b, n, send, 0)
+    arrived(e_l, nl, send, 0)
+    arrived(e_b, nb, send, last - 1)
     for h in range(halves):
         arrived(b_b.at[h], n, send, 1 + h)
         arrived(r_a.at[h], n, send, 1 + halves + h)
@@ -288,6 +366,7 @@
     f32 = jnp.float32
     state = pltpu.VMEM((halves, n, 2, per // halves, lanes), f32)
     level = pltpu.VMEM((n, per, lanes), f32)
+    spread = pltpu.VMEM((nb, nl, per, lanes), f32)
     vmem = pl.BlockSpec(memory_space=pltpu.VMEM)
     anywhere = pl.BlockSpec(memory_space=pl.ANY)
     whole = pltpu.VMEM((2, depth, rows, lanes), f32)
@@ -295,14 +374,17 @@
         functools.partial(kernel, nb, nl, halves),
         name="register",
         out_shape=(pltpu.VMEM(amplitudes.shape, f32), pltpu.VMEM((depth, piece, lanes), f32)),
-        in_specs=[anywhere, anywhere, vmem, vmem],
+        in_specs=[anywhere] * 4,
         out_specs=(vmem, vmem),
         scratch_shapes=[
+            pltpu.VMEM(phase_angles.shape, f32),
+            pltpu.VMEM(mix_angles.shape, f32),
             whole,
-            level,
+            spread,
+            pltpu.VMEM((nl, nb, per, lanes), f32),
             whole if per % 8 else pltpu.VMEM((1, 1, 8, 128), f32),
             state,
-            level,
+            spread,
             state,
             state,
             state,
@@ -311,12 +393,15 @@
             pltpu.VMEM((2, depth, rows // halves, lanes), f32),
             pltpu.VMEM((depth, nb, piece, lanes), f32),
             pltpu.VMEM((nb, depth, piece, lanes), f32),
-            pltpu.SemaphoreType.DMA((2,)),
-            pltpu.SemaphoreType.DMA((2 * halves + 2,)),
-            pltpu.SemaphoreType.DMA((2 * halves + 2,)),
+            pltpu.SemaphoreType.DMA((4,)),
+            pltpu.SemaphoreType.DMA((2 * halves + 3,)),
+            pltpu.SemaphoreType.DMA((2 * halves + 3,)),
+            pltpu.SemaphoreType.REGULAR,
+            pltpu.SemaphoreType.REGULAR,
+            pltpu.SemaphoreType.REGULAR,
         ],
         compiler_params=pltpu.CompilerParams(collective_id=0, has_side_effects=True),
-    )(amplitudes, energies.reshape(n, per, lanes), phase_angles, mix_angles)
+    )(amplitudes, energies.reshape(nb, nl, per, lanes), phase_angles, mix_angles)
 
 
 def solution(mesh):

time: 43.6 us -> 42.5 us (0.975)
  the two profiles are of different devices: /device:TPU:9 before, /device:TPU:0 now
where the time goes in v1:
time: 42.5 us; the launch traced here: 42.3 us
  Pallas kernels  40.3 us (95%)
  local copies, waits for them, and re-layouts  1.41 us (3%)
  between operations  0.64 us (2%)
    pallas_call x1, Pallas kernels, on_device(): pl.pallas_call(functools.partial(kernel, nb, nl, halves), name='register'...  40.3 us
    unnamed x2, local copies, waits for them, and re-layouts  1.41 us

profile of v1, /device:TPU:0, one launch (start us, length us, event | category | flops | bytes accessed | tf_op | source)
XLA Modules:
  0.0 42.3 jit_solution(16161349974514811004)
XLA Ops:
  0.6 40.3 %register.1 = (f32[2,4,128,128]{3,2,1,0:T(8,128)S(1)}, f32[4,16,128]{2,1,0:T(8,128)S(1)}) custom-call(f32[2,4,128,128]{3,2,1,0:T(8,128)} %amp_hbm.1, f32[8,4,16,128]{3,2,1,0:T(8,128)} %bitcast.1, f32[2,128]{1,0:T(2,128)} %ph_hbm.1, f32[2,4]{1,0:T(2,128)} %mix_hbm.1), custom_call_target="tpu_custom_call" | custom-call | tf_op jit(solution)/shard_map/register/pallas_call | solution.py:373
  40.9 0.8 %copy.8 = f32[2,4,128,128]{3,2,1,0:T(8,128)} copy(f32[2,4,128,128]{3,2,1,0:T(8,128)S(1)} %get-tuple-element.2) | data formatting | bytes 1048576
  41.7 0.6 %copy.9 = f32[4,16,128]{2,1,0:T(8,128)} copy(f32[4,16,128]{2,1,0:T(8,128)S(1)} %get-tuple-element.3) | data formatting | bytes 65536

commit v2 on v1

--- a/solution.py
+++ b/solution.py
@@ -36,16 +36,18 @@
     return one(a[0], b[0]) + (one(a[1], b[0]) + one(a[0], b[1]))
 
 
-def turn_table(count, cosine, sine):
+def turn_table(count, cosine, sine, places=None):
+    places = count.bit_length() - 1 if places is None else places
     row = lax.broadcasted_iota(jnp.int32, (count, count), 0)
     col = lax.broadcasted_iota(jnp.int32, (count, count), 1)
     apart = row ^ col
     size = jnp.ones((count, count), jnp.float32)
     ones = jnp.zeros((count, count), jnp.int32)
-    for place in range(count.bit_length() - 1):
+    for place in range(places):
         bit = (apart >> place) & 1
         size = size * jnp.where(bit == 1, sine, cosine)
         ones = ones + bit
+    size = jnp.where(apart >> places == 0, size, 0.0)
     phase = ones & 3
     real = jnp.where(phase == 0, size, jnp.where(phase == 2, -size, 0.0))
     imag = jnp.where(phase == 1, -size, jnp.where(phase == 3, size, 0.0))
@@ -357,12 +359,335 @@
     arrived(m_in, nb, send, last)
 
 
+def contact(nb, nl, bank, lane, line_in, lines_in, all_in):
+    barrier = pltpu.get_barrier_semaphore()
+    hub = nl // 2 - 1
+
+    def signal_hubs(sem):
+        def one(k, carry):
+            pl.semaphore_signal(sem, 1, device_id=(lax.rem(bank + k, nb), hub), device_id_type=MESH)
+            return carry
+
+        lax.fori_loop(1, nb, one, 0)
+
+    def greet():
+        def one(k, carry):
+            to = lax.rem(lane + k, nl)
+
+            @pl.when(to != hub)
+            def _():
+                pl.semaphore_signal(barrier, 1, device_id=(bank, to), device_id_type=MESH)
+
+            return carry
+
+        @pl.when(lane == hub)
+        def _():
+            signal_hubs(barrier)
+
+        lax.fori_loop(1, nl, one, 0)
+
+    def line():
+        pl.semaphore_wait(barrier, jnp.where(lane == hub, nb - 1, nl - 1))
+
+        @pl.when(lane == hub + 1)
+        def _():
+            pl.semaphore_signal(line_in, 1, device_id=(bank, hub), device_id_type=MESH)
+
+        @pl.when(lane == hub)
+        def _():
+            pl.semaphore_wait(line_in, 1)
+            signal_hubs(lines_in)
+
+    def everyone():
+        @pl.when(lane == hub)
+        def _():
+            pl.semaphore_wait(lines_in, nb - 1)
+
+            def tell(k, carry):
+                pl.semaphore_signal(all_in, 1, device_id=(bank, lax.rem(lane + k, nl)), device_id_type=MESH)
+                return carry
+
+            lax.fori_loop(1, nl, tell, 0)
+
+        @pl.when(lane != hub)
+        def _():
+            pl.semaphore_wait(all_in, 1)
+
+    return greet, line, everyone
+
+
+def pieces(
+    nb, nl, amp_hbm, en_hbm, ph_hbm, mix_hbm, out, marg,
+    ph, mix, amp, en, e_l, s_a, e_b, b_b, o_a, o_b, r_a, r_b, cs_b, sn_b, part, ch, m_in,
+    load, send, recv, line_in, lines_in, all_in,
+):
+    n = nb * nl
+    depth, rows, lanes = amp.shape[1:]
+    step = s_a.shape[3]
+    half = step // 2
+    units = rows // (2 * step)
+    bank, lane = lax.axis_index("bank"), lax.axis_index("lane")
+    me = bank * nl + lane
+    greet, line, everyone = contact(nb, nl, bank, lane, line_in, lines_in, all_in)
+    loads = [
+        pltpu.make_async_copy(x, y, load.at[i])
+        for i, (x, y) in enumerate([(en_hbm, en), (mix_hbm, mix), (amp_hbm, amp), (ph_hbm, ph)])
+    ]
+    greet()
+    for copy in loads:
+        copy.start()
+
+    def remote(src, dst, which, to):
+        pltpu.make_async_remote_copy(
+            src_ref=src,
+            dst_ref=dst,
+            send_sem=send.at[which],
+            recv_sem=recv.at[which],
+            device_id=to,
+            device_id_type=MESH,
+        ).start()
+
+    def exchange(src, dst, which, ahead=False):
+        def one(k, carry):
+            to_bank, apart = lax.rem(bank + nb - lax.rem(k, nb), nb), k // nb
+            if ahead:
+                to_lane = apart
+            else:
+                to_lane = apart
+
+            @pl.when(to_bank * nl + to_lane != me)
+            def _():
+                remote(src.at[to_bank * nl + to_lane], dst.at[me], which, (to_bank, to_lane))
+
+            return carry
+
+        lax.fori_loop(0, n, one, 0)
+        dst[me] = src[me]
+
+    def along_line(src, dst, which):
+        def one(k, carry):
+            to = lane ^ (nl - k)
+            remote(src.at[:, to], dst.at[lane], which, (bank, to))
+            return carry
+
+        lax.fori_loop(1, nl, one, 0)
+        dst[lane] = src[:, lane]
+
+    def across(pick, dst, which):
+        def one(to, carry):
+            @pl.when(to != bank)
+            def _():
+                remote(pick(to), dst.at[bank], which, (to, lane))
+
+            return carry
+
+        lax.fori_loop(0, nb, one, 0)
+
+    def arrived(dst, count, sems, which):
+        most = dst.at[pl.ds(0, count - 1)]
+        pltpu.make_async_copy(most, most, sems.at[which]).wait()
+
+    def angle(layer, group):
+        return cosines[layer : layer + 1, group : group + 1], sines[layer : layer + 1, group : group + 1]
+
+    def mixed(layer, re, im, stride, stop, group):
+        cosine, sine = (jnp.broadcast_to(x, re.shape[1:])[None, None] for x in angle(layer, group))
+        while stride < stop:
+            re, im = butterfly(re, im, stride, cosine, sine)
+            stride *= 2
+        return re, im
+
+    def lane_table(layer):
+        real, imag = turn_table(lanes, *angle(layer, 0))
+        return split(jnp.concatenate([jnp.concatenate([real, imag], 1), jnp.concatenate([-imag, real], 1)], 0))
+
+    def row_table(layer, count, places=None):
+        real, imag = turn_table(count, *angle(layer, 1), places)
+        return split(jnp.concatenate([jnp.concatenate([real, -imag], 1), jnp.concatenate([imag, real], 1)], 0))
+
+    loads[0].wait()
+    line()
+    along_line(en, e_l, 0)
+    loads[1].wait()
+    cosines, sines = jnp.cos(mix[...]), jnp.sin(mix[...])
+    lane_first, row_first = lane_table(0), row_table(0, rows)
+    lane_second, row_second = lane_table(1), row_table(1, lanes, step.bit_length() - 1)
+    loads[2].wait()
+    loads[3].wait()
+
+    pairs = []
+    for d in range(depth):
+        e = en[pl.ds(d * units // nl, units // nl)].reshape(rows, lanes)
+        sine, cosine = sin_cos(ph[0:1] * e)
+        pairs.append((amp[0, d] * cosine + amp[1, d] * sine, amp[1, d] * cosine - amp[0, d] * sine))
+    re = jnp.stack([p[0] for p in pairs]).reshape(depth, rows // 8, 8, lanes)
+    im = jnp.stack([p[1] for p in pairs]).reshape(depth, rows // 8, 8, lanes)
+    cosine, sine = (jnp.broadcast_to(x, (8, lanes))[None] for x in angle(0, 2))
+    stride = 1
+    while stride < depth:
+        re, im = butterfly(re, im, stride, cosine, sine)
+        stride *= 2
+    re, im = re.reshape(depth, rows, lanes), im.reshape(depth, rows, lanes)
+    for d in range(depth):
+        both = dot3(split(jnp.concatenate([re[d], im[d]], 1)), lane_first)
+        both = dot3(row_first, split(jnp.concatenate([both[:, :lanes], both[:, lanes:]], 0)))
+        for i in range(2):
+            x = both[i * rows : (i + 1) * rows].reshape(units, 2, step, lanes)
+            for h in range(2):
+                s_a[h, pl.ds(d * units, units), i] = x[:, h]
+
+    everyone()
+    exchange(s_a.at[0], b_b.at[0], 2)
+    arrived(e_l, nl, recv, 0)
+    across(lambda to: e_l.at[:, to], e_b, 1)
+    e_b[bank] = e_l[:, bank]
+    exchange(s_a.at[1], b_b.at[1], 3)
+    arrived(e_b, nb, recv, 1)
+    sine, cosine = sin_cos(ph[1:2][None] * e_b[...].reshape(n, 2 * step, lanes))
+    sn_b[...] = sine
+    cs_b[...] = cosine
+
+    for h in range(2):
+        arrived(b_b.at[h], n, recv, 2 + h)
+        span = pl.ds(h * step, step)
+        re, im = b_b[h, :, 0], b_b[h, :, 1]
+        re, im = mixed(0, re, im, 1, nl, 3)
+        re, im = mixed(0, re, im, nl, n, 2)
+        cosine, sine = cs_b[:, span], sn_b[:, span]
+        re, im = re * cosine + im * sine, im * cosine - re * sine
+        re, im = mixed(1, re, im, 1, nl, 3)
+        re, im = mixed(1, re, im, nl, n, 2)
+        re, im = re.reshape(n * step, lanes), im.reshape(n * step, lanes)
+        both = dot3(split(jnp.concatenate([re, im], 1)), lane_second)
+        groups = range(0, n * step, lanes)
+        wide = [jnp.concatenate([both[g : g + lanes, i * lanes : (i + 1) * lanes] for g in groups], 1) for i in range(2)]
+        both = dot3(row_second, split(jnp.concatenate(wide, 0)))
+        for i in range(2):
+            x = [both[i * lanes : (i + 1) * lanes, g : g + lanes] for g in groups]
+            x = jnp.concatenate(x, 0).reshape(n, step, lanes)
+            if h == 0:
+                o_a[:, i] = x
+            else:
+                for s in range(2):
+                    o_b[s, :, i] = x[:, s * half : (s + 1) * half]
+        if h == 0:
+            exchange(o_a, r_a, 4, True)
+        else:
+            for s in range(2):
+                exchange(o_b.at[s], r_b.at[s], 5 + s, True)
+
+    arrived(r_a, n, recv, 4)
+    re, im = mixed(1, r_a[:, 0], r_a[:, 1], 1, units, 1)
+    re, im = mixed(1, re, im, units, n, 2)
+    for s in range(2):
+        part[s, 0] = re[:, s * half : (s + 1) * half]
+        part[s, 1] = im[:, s * half : (s + 1) * half]
+
+    for s in range(2):
+        arrived(r_b.at[s], n, recv, 5 + s)
+        vr, vi = mixed(1, r_b[s, :, 0], r_b[s, :, 1], 1, units, 1)
+        vr, vi = mixed(1, vr, vi, units, n, 2)
+        ur, ui = part[s, 0], part[s, 1]
+        cosine, sine = (jnp.broadcast_to(x, (half, lanes))[None] for x in angle(1, 1))
+        re = (cosine * ur + sine * vi, cosine * vr + sine * ui)
+        im = (cosine * ui - sine * vr, cosine * vi - sine * ur)
+        for h in range(2):
+            chance = re[h] * re[h] + im[h] * im[h]
+            for d in range(depth):
+                ch[s, :, d, h] = chance[d * units : (d + 1) * units]
+        across(lambda to: ch.at[s, to], m_in.at[s], 7 + s)
+        m_in[s, bank] = ch[s, bank]
+        for h in range(2):
+            for i, x in enumerate((re[h], im[h])):
+                out[i, :, :, h, s * half : (s + 1) * half] = x.reshape(depth, units, half, lanes)
+
+    for s in range(2):
+        arrived(m_in.at[s], nb, recv, 7 + s)
+        total = m_in[s, 0]
+        for g in range(1, nb):
+            total = total + m_in[s, g]
+        marg[:, :, s * half : (s + 1) * half] = total * (1.0 / nb)
+    arrived(e_l, nl, send, 0)
+    arrived(e_b, nb, send, 1)
+    for h in range(2):
+        arrived(b_b.at[h], n, send, 2 + h)
+        arrived(r_b.at[h], n, send, 5 + h)
+        arrived(m_in.at[h], nb, send, 7 + h)
+    arrived(r_a, n, send, 4)
+
+
+def keep(a, b, a_hbm, b_hbm, sems):
+    copies = [pltpu.make_async_copy(a, a_hbm, sems.at[0]), pltpu.make_async_copy(b, b_hbm, sems.at[1])]
+    for copy in copies:
+        copy.start()
+    for copy in copies:
+        copy.wait()
+
+
+def in_pieces(nb, nl, amplitudes, energies, phase_angles, mix_angles):
+    _, depth, rows, lanes = amplitudes.shape
+    n = nb * nl
+    per = depth * rows // n
+    step, half = per // 2, per // 4
+    f32 = jnp.float32
+    vmem = pl.BlockSpec(memory_space=pltpu.VMEM)
+    anywhere = pl.BlockSpec(memory_space=pl.ANY)
+    state = pltpu.VMEM((2, n, 2, step, lanes), f32)
+    level = pltpu.VMEM((n, per, lanes), f32)
+    spread = pltpu.VMEM((nb, nl, per, lanes), f32)
+    shapes = (2, depth, nb, 2, step, lanes), (depth, 2, step, lanes)
+    results = pl.pallas_call(
+        functools.partial(pieces, nb, nl),
+        name="register",
+        out_shape=tuple(pltpu.VMEM(shape, f32) for shape in shapes),
+        in_specs=[anywhere] * 4,
+        out_specs=(vmem, vmem),
+        scratch_shapes=[
+            pltpu.VMEM(phase_angles.shape, f32),
+            pltpu.VMEM(mix_angles.shape, f32),
+            pltpu.VMEM((2, depth, rows, lanes), f32),
+            spread,
+            pltpu.VMEM((nl, nb, per, lanes), f32),
+            state,
+            spread,
+            state,
+            pltpu.VMEM((n, 2, step, lanes), f32),
+            pltpu.VMEM((2, n, 2, half, lanes), f32),
+            pltpu.VMEM((n, 2, step, lanes), f32),
+            pltpu.VMEM((2, n, 2, half, lanes), f32),
+            level,
+            level,
+            pltpu.VMEM((2, 2, n, half, lanes), f32),
+            pltpu.VMEM((2, nb, depth, 2, half, lanes), f32),
+            pltpu.VMEM((2, nb, depth, 2, half, lanes), f32),
+            pltpu.SemaphoreType.DMA((4,)),
+            pltpu.SemaphoreType.DMA((9,)),
+            pltpu.SemaphoreType.DMA((9,)),
+            pltpu.SemaphoreType.REGULAR,
+            pltpu.SemaphoreType.REGULAR,
+            pltpu.SemaphoreType.REGULAR,
+        ],
+        compiler_params=pltpu.CompilerParams(collective_id=0, has_side_effects=True),
+    )(amplitudes, energies.reshape(nb, nl, per, lanes), phase_angles, mix_angles)
+    final, marginal = pl.pallas_call(
+        keep,
+        name="keep",
+        out_shape=tuple(jax.ShapeDtypeStruct(shape, f32) for shape in shapes),
+        in_specs=[vmem, vmem],
+        out_specs=(anywhere, anywhere),
+        scratch_shapes=[pltpu.SemaphoreType.DMA((2,))],
+    )(*[pltpu.with_memory_space_constraint(x, pltpu.VMEM) for x in results])
+    return final.reshape(amplitudes.shape), marginal.reshape(depth, rows // nb, lanes)
+
+
 def on_device(nb, nl, amplitudes, energies, phase_angles, mix_angles):
     _, depth, rows, lanes = amplitudes.shape
     n = nb * nl
     per = depth * rows // n
     halves = 2 if per % 16 == 0 else 1
     piece = rows // nb
+    if per == 2 * 8 and piece == per and rows // per % nl == 0 and n * 8 % lanes == 0:
+        return in_pieces(nb, nl, amplitudes, energies, phase_angles, mix_angles)
     f32 = jnp.float32
     state = pltpu.VMEM((halves, n, 2, per // halves, lanes), f32)
     level = pltpu.VMEM((n, per, lanes), f32)

time: 42.5 us -> 40.5 us (0.953)
  the two profiles are of different devices: /device:TPU:0 before, /device:TPU:25 now
where the time goes in v2:
time: 40.5 us; the launch traced here: 40.3 us
  Pallas kernels  39.7 us (98%)
  between operations  0.64 us (2%)
    pallas_call x1, Pallas kernels, in_pieces(): pl.pallas_call(functools.partial(pieces, nb, nl), name='register', out_sh...  38.9 us
    pallas_call x1, Pallas kernels, in_pieces(): pl.pallas_call(keep, name='keep', out_shape=tuple((jax.ShapeDtypeStruct(s...  0.81 us

profile of v2, /device:TPU:25, one launch (start us, length us, event | category | flops | bytes accessed | tf_op | source)
XLA Modules:
  0.0 40.3 jit_solution(4208557244274389850)
XLA Ops:
  0.6 38.9 %register.1 = (f32[2,4,8,2,8,128]{5,4,3,2,1,0:T(8,128)S(1)}, f32[4,2,8,128]{3,2,1,0:T(8,128)S(1)}) custom-call(f32[2,4,128,128]{3,2,1,0:T(8,128)} %amp_hbm.1, f32[8,4,16,128]{3,2,1,0:T(8,128)} %bitcast.3, f32[2,128]{1,0:T(2,128)} %ph_hbm.1, f32[2,4]{1,0:T(2,128)} %mix_hbm.1), custom_call_target="tpu_custom_call" | custom-call | tf_op jit(solution)/shard_map/register/pallas_call | solution.py:639
  39.5 0.8 %keep.1 = (f32[2,4,8,2,8,128]{5,4,3,2,1,0:T(8,128)}, f32[4,2,8,128]{3,2,1,0:T(8,128)}) custom-call(f32[2,4,8,2,8,128]{5,4,3,2,1,0:T(8,128)S(1)} %get-tuple-element.6.a, f32[4,2,8,128]{3,2,1,0:T(8,128)S(1)} %get-tuple-element.7.b), custom_call_target="tpu_custom_call" | custom-call | tf_op jit(solution)/shard_map/keep/pallas_call | solution.py:672

commit v3 on v2

--- a/solution.py
+++ b/solution.py
@@ -359,67 +359,79 @@
     arrived(m_in, nb, send, last)
 
 
-def contact(nb, nl, bank, lane, line_in, lines_in, all_in):
+def contact(nb, nl, bank, lane, line_in, last_in, lines_in, all_in):
     barrier = pltpu.get_barrier_semaphore()
-    hub = nl // 2 - 1
+    last = nl - 1
+    is_hub, is_last = lane == 0, lane == last
+    between = jnp.logical_not(jnp.logical_or(is_hub, is_last))
+
+    def signal(sem, to_bank, to_lane):
+        pl.semaphore_signal(sem, 1, device_id=(to_bank, to_lane), device_id_type=MESH)
 
     def signal_hubs(sem):
         def one(k, carry):
-            pl.semaphore_signal(sem, 1, device_id=(lax.rem(bank + k, nb), hub), device_id_type=MESH)
+            signal(sem, lax.rem(bank + k, nb), 0)
             return carry
 
         lax.fori_loop(1, nb, one, 0)
 
     def greet():
-        def one(k, carry):
-            to = lax.rem(lane + k, nl)
-
-            @pl.when(to != hub)
-            def _():
-                pl.semaphore_signal(barrier, 1, device_id=(bank, to), device_id_type=MESH)
-
-            return carry
-
-        @pl.when(lane == hub)
+        @pl.when(is_last)
+        def _():
+            signal(barrier, bank, 0)
+
+        @pl.when(jnp.logical_not(is_last))
+        def _():
+            for to in range(last, 0, -1):
+
+                @pl.when(lane != to)
+                def _():
+                    signal(barrier, bank, to)
+
+        @pl.when(is_hub)
         def _():
             signal_hubs(barrier)
 
-        lax.fori_loop(1, nl, one, 0)
-
     def line():
-        pl.semaphore_wait(barrier, jnp.where(lane == hub, nb - 1, nl - 1))
-
-        @pl.when(lane == hub + 1)
-        def _():
-            pl.semaphore_signal(line_in, 1, device_id=(bank, hub), device_id_type=MESH)
-
-        @pl.when(lane == hub)
+        pl.semaphore_wait(barrier, jnp.where(is_hub, nb, jnp.where(is_last, last, last - 1)))
+
+        @pl.when(lane == 1)
+        def _():
+            signal(line_in, bank, 0)
+
+        @pl.when(is_hub)
         def _():
             pl.semaphore_wait(line_in, 1)
+            for to in range(1, last):
+                signal(last_in, bank, to)
             signal_hubs(lines_in)
 
+    def all_of_line():
+        @pl.when(between)
+        def _():
+            pl.semaphore_wait(last_in, 1)
+
     def everyone():
-        @pl.when(lane == hub)
+        @pl.when(is_hub)
         def _():
             pl.semaphore_wait(lines_in, nb - 1)
-
-            def tell(k, carry):
-                pl.semaphore_signal(all_in, 1, device_id=(bank, lax.rem(lane + k, nl)), device_id_type=MESH)
-                return carry
-
-            lax.fori_loop(1, nl, tell, 0)
-
-        @pl.when(lane != hub)
+            for to in range(last, 0, -1):
+                signal(all_in, bank, to)
+
+        @pl.when(jnp.logical_not(is_hub))
         def _():
             pl.semaphore_wait(all_in, 1)
 
-    return greet, line, everyone
+    def known(to):
+        return jnp.logical_not(jnp.logical_and(between, to == last))
+
+    return greet, line, all_of_line, everyone, known
 
 
 def pieces(
     nb, nl, amp_hbm, en_hbm, ph_hbm, mix_hbm, out, marg,
     ph, mix, amp, en, e_l, s_a, e_b, b_b, o_a, o_b, r_a, r_b, cs_b, sn_b, part, ch, m_in,
-    load, send, recv, line_in, lines_in, all_in,
+    load, send, recv, *met,
 ):
     n = nb * nl
     depth, rows, lanes = amp.shape[1:]
@@ -428,7 +440,7 @@
     units = rows // (2 * step)
     bank, lane = lax.axis_index("bank"), lax.axis_index("lane")
     me = bank * nl + lane
-    greet, line, everyone = contact(nb, nl, bank, lane, line_in, lines_in, all_in)
+    greet, line, all_of_line, everyone, known = contact(nb, nl, bank, lane, *met)
     loads = [
         pltpu.make_async_copy(x, y, load.at[i])
         for i, (x, y) in enumerate([(en_hbm, en), (mix_hbm, mix), (amp_hbm, amp), (ph_hbm, ph)])
@@ -447,13 +459,9 @@
             device_id_type=MESH,
         ).start()
 
-    def exchange(src, dst, which, ahead=False):
+    def send_lane(to_lane, src, dst, which):
         def one(k, carry):
-            to_bank, apart = lax.rem(bank + nb - lax.rem(k, nb), nb), k // nb
-            if ahead:
-                to_lane = apart
-            else:
-                to_lane = apart
+            to_bank = lax.rem(bank + k, nb)
 
             @pl.when(to_bank * nl + to_lane != me)
             def _():
@@ -461,17 +469,34 @@
 
             return carry
 
-        lax.fori_loop(0, n, one, 0)
+        lax.fori_loop(0, nb, one, 0)
+
+    def now(to):
+        return jnp.logical_or(lane != 2, to != 1)
+
+    def exchange(src, dst, which):
+        def one(to_lane, carry):
+            send_lane(to_lane, src, dst, which)
+            return carry
+
+        lax.fori_loop(0, nl, one, 0)
         dst[me] = src[me]
 
-    def along_line(src, dst, which):
-        def one(k, carry):
-            to = lane ^ (nl - k)
-            remote(src.at[:, to], dst.at[lane], which, (bank, to))
-            return carry
-
-        lax.fori_loop(1, nl, one, 0)
-        dst[lane] = src[:, lane]
+    def along_line(k, start):
+        to = lane ^ (nl - k)
+        copy = pltpu.make_async_remote_copy(
+            src_ref=en.at[:, to],
+            dst_ref=e_l.at[lane if start else to],
+            send_sem=send.at[8 + k],
+            recv_sem=recv.at[8 + k],
+            device_id=(bank, to),
+            device_id_type=MESH,
+        )
+        if start:
+            copy.start()
+            return None
+        copy.wait_recv()
+        return to
 
     def across(pick, dst, which):
         def one(to, carry):
@@ -507,7 +532,8 @@
 
     loads[0].wait()
     line()
-    along_line(en, e_l, 0)
+    for k in range(1, nl):
+        pl.when(known(lane ^ (nl - k)))(functools.partial(along_line, k, True))
     loads[1].wait()
     cosines, sines = jnp.cos(mix[...]), jnp.sin(mix[...])
     lane_first, row_first = lane_table(0), row_table(0, rows)
@@ -536,11 +562,17 @@
             for h in range(2):
                 s_a[h, pl.ds(d * units, units), i] = x[:, h]
 
+    all_of_line()
+    for k in range(1, nl):
+        pl.when(jnp.logical_not(known(lane ^ (nl - k))))(functools.partial(along_line, k, True))
     everyone()
+    across(lambda to: en.at[to, lane], e_b.at[:, lane], 1)
+    e_b[bank, lane] = en[bank, lane]
     exchange(s_a.at[0], b_b.at[0], 2)
-    arrived(e_l, nl, recv, 0)
-    across(lambda to: e_l.at[:, to], e_b, 1)
-    e_b[bank] = e_l[:, bank]
+    for k in range(1, nl):
+        source = along_line(k, False)
+        across(lambda to: e_l.at[source, to], e_b.at[:, source], 1)
+        e_b[bank, source] = e_l[source, bank]
     exchange(s_a.at[1], b_b.at[1], 3)
     arrived(e_b, nb, recv, 1)
     sine, cosine = sin_cos(ph[1:2][None] * e_b[...].reshape(n, 2 * step, lanes))
@@ -571,10 +603,17 @@
                 for s in range(2):
                     o_b[s, :, i] = x[:, s * half : (s + 1) * half]
         if h == 0:
-            exchange(o_a, r_a, 4, True)
+            for to in [0, 3, 1, 2]:
+                pl.when(now(to))(functools.partial(send_lane, to, o_a, r_a, 4))
+            r_a[me] = o_a[me]
         else:
+            for to, s in [(0, 0), (3, 0), (0, 1), (3, 1), (1, -1), (1, 0), (2, 0), (1, 1), (2, 1)]:
+                if s < 0:
+                    pl.when(jnp.logical_not(now(to)))(functools.partial(send_lane, to, o_a, r_a, 4))
+                else:
+                    send_lane(to, o_b.at[s], r_b.at[s], 5 + s)
             for s in range(2):
-                exchange(o_b.at[s], r_b.at[s], 5 + s, True)
+                r_b[s, me] = o_b[s, me]
 
     arrived(r_a, n, recv, 4)
     re, im = mixed(1, r_a[:, 0], r_a[:, 1], 1, units, 1)
@@ -595,24 +634,25 @@
             chance = re[h] * re[h] + im[h] * im[h]
             for d in range(depth):
                 ch[s, :, d, h] = chance[d * units : (d + 1) * units]
-        across(lambda to: ch.at[s, to], m_in.at[s], 7 + s)
+        across(lambda to: ch.at[s, to], m_in.at[s], 7 * s)
         m_in[s, bank] = ch[s, bank]
         for h in range(2):
             for i, x in enumerate((re[h], im[h])):
                 out[i, :, :, h, s * half : (s + 1) * half] = x.reshape(depth, units, half, lanes)
 
     for s in range(2):
-        arrived(m_in.at[s], nb, recv, 7 + s)
+        arrived(m_in.at[s], nb, recv, 7 * s)
         total = m_in[s, 0]
         for g in range(1, nb):
             total = total + m_in[s, g]
         marg[:, :, s * half : (s + 1) * half] = total * (1.0 / nb)
-    arrived(e_l, nl, send, 0)
+    for k in range(1, nl):
+        pltpu.make_async_copy(en.at[:, 0], e_l.at[0], send.at[8 + k]).wait()
     arrived(e_b, nb, send, 1)
     for h in range(2):
         arrived(b_b.at[h], n, send, 2 + h)
         arrived(r_b.at[h], n, send, 5 + h)
-        arrived(m_in.at[h], nb, send, 7 + h)
+        arrived(m_in.at[h], nb, send, 7 * h)
     arrived(r_a, n, send, 4)
 
 
@@ -661,11 +701,9 @@
             pltpu.VMEM((2, nb, depth, 2, half, lanes), f32),
             pltpu.VMEM((2, nb, depth, 2, half, lanes), f32),
             pltpu.SemaphoreType.DMA((4,)),
-            pltpu.SemaphoreType.DMA((9,)),
-            pltpu.SemaphoreType.DMA((9,)),
-            pltpu.SemaphoreType.REGULAR,
-            pltpu.SemaphoreType.REGULAR,
-            pltpu.SemaphoreType.REGULAR,
+            pltpu.SemaphoreType.DMA((8 + nl,)),
+            pltpu.SemaphoreType.DMA((8 + nl,)),
+            *[pltpu.SemaphoreType.REGULAR] * 4,
         ],
         compiler_params=pltpu.CompilerParams(collective_id=0, has_side_effects=True),
     )(amplitudes, energies.reshape(nb, nl, per, lanes), phase_angles, mix_angles)

time: 40.5 us -> 39.5 us (0.975)
  the two profiles are of different devices: /device:TPU:25 before, /device:TPU:9 now
where the time goes in v3:
time: 39.5 us; the launch traced here: 39.2 us
  Pallas kernels  38.6 us (98%)
  between operations  0.64 us (2%)
    pallas_call x1, Pallas kernels, in_pieces(): pl.pallas_call(functools.partial(pieces, nb, nl), name='register', out_sh...  37.7 us
    pallas_call x1, Pallas kernels, in_pieces(): pl.pallas_call(keep, name='keep', out_shape=tuple((jax.ShapeDtypeStruct(s...  0.81 us

profile of v3, /device:TPU:9, one launch (start us, length us, event | category | flops | bytes accessed | tf_op | source)
XLA Modules:
  0.0 39.2 jit_solution(17568661081508889894)
XLA Ops:
  0.6 37.7 %register.1 = (f32[2,4,8,2,8,128]{5,4,3,2,1,0:T(8,128)S(1)}, f32[4,2,8,128]{3,2,1,0:T(8,128)S(1)}) custom-call(f32[2,4,128,128]{3,2,1,0:T(8,128)} %amp_hbm.1, f32[8,4,16,128]{3,2,1,0:T(8,128)} %bitcast.3, f32[2,128]{1,0:T(2,128)} %ph_hbm.1, f32[2,4]{1,0:T(2,128)} %mix_hbm.1), custom_call_target="tpu_custom_call" | custom-call | tf_op jit(solution)/shard_map/register/pallas_call | solution.py:679
  38.4 0.8 %keep.1 = (f32[2,4,8,2,8,128]{5,4,3,2,1,0:T(8,128)}, f32[4,2,8,128]{3,2,1,0:T(8,128)}) custom-call(f32[2,4,8,2,8,128]{5,4,3,2,1,0:T(8,128)S(1)} %get-tuple-element.6.a, f32[4,2,8,128]{3,2,1,0:T(8,128)S(1)} %get-tuple-element.7.b), custom_call_target="tpu_custom_call" | custom-call | tf_op jit(solution)/shard_map/keep/pallas_call | solution.py:710

commit v4 on v3

--- a/solution.py
+++ b/solution.py
@@ -430,7 +430,7 @@
 
 def pieces(
     nb, nl, amp_hbm, en_hbm, ph_hbm, mix_hbm, out, marg,
-    ph, mix, amp, en, e_l, s_a, e_b, b_b, o_a, o_b, r_a, r_b, cs_b, sn_b, part, ch, m_in,
+    ph, mix, amp, en, e_l, s_a, e_b, b_b, o_a, o_b, r_a, r_b, cs_b, sn_b, part, ch, near, pair, m_in,
     load, send, recv, *met,
 ):
     n = nb * nl
@@ -440,6 +440,7 @@
     units = rows // (2 * step)
     bank, lane = lax.axis_index("bank"), lax.axis_index("lane")
     me = bank * nl + lane
+    side, pairs_at = lax.rem(bank, 2), bank // 2
     greet, line, all_of_line, everyone, known = contact(nb, nl, bank, lane, *met)
     loads = [
         pltpu.make_async_copy(x, y, load.at[i])
@@ -474,12 +475,9 @@
     def now(to):
         return jnp.logical_or(lane != 2, to != 1)
 
-    def exchange(src, dst, which):
-        def one(to_lane, carry):
-            send_lane(to_lane, src, dst, which)
-            return carry
-
-        lax.fori_loop(0, nl, one, 0)
+    def exchange(src, dst, which, order):
+        for to in order:
+            send_lane(to, src, dst, which)
         dst[me] = src[me]
 
     def along_line(k, start):
@@ -568,12 +566,12 @@
     everyone()
     across(lambda to: en.at[to, lane], e_b.at[:, lane], 1)
     e_b[bank, lane] = en[bank, lane]
-    exchange(s_a.at[0], b_b.at[0], 2)
+    exchange(s_a.at[0], b_b.at[0], 2, (1, 2, 0, 3))
     for k in range(1, nl):
         source = along_line(k, False)
         across(lambda to: e_l.at[source, to], e_b.at[:, source], 1)
         e_b[bank, source] = e_l[source, bank]
-    exchange(s_a.at[1], b_b.at[1], 3)
+    exchange(s_a.at[1], b_b.at[1], 3, (1, 2, 0, 3))
     arrived(e_b, nb, recv, 1)
     sine, cosine = sin_cos(ph[1:2][None] * e_b[...].reshape(n, 2 * step, lanes))
     sn_b[...] = sine
@@ -603,11 +601,11 @@
                 for s in range(2):
                     o_b[s, :, i] = x[:, s * half : (s + 1) * half]
         if h == 0:
-            for to in [0, 3, 1, 2]:
+            for to in [0,2,1,3]:
                 pl.when(now(to))(functools.partial(send_lane, to, o_a, r_a, 4))
             r_a[me] = o_a[me]
         else:
-            for to, s in [(0, 0), (3, 0), (0, 1), (3, 1), (1, -1), (1, 0), (2, 0), (1, 1), (2, 1)]:
+            for to, s in [(0,0),(2,0),(0,1),(2,1),(1,-1),(1,0),(3,0),(1,1),(3,1)]:
                 if s < 0:
                     pl.when(jnp.logical_not(now(to)))(functools.partial(send_lane, to, o_a, r_a, 4))
                 else:
@@ -633,17 +631,29 @@
         for h in range(2):
             chance = re[h] * re[h] + im[h] * im[h]
             for d in range(depth):
-                ch[s, :, d, h] = chance[d * units : (d + 1) * units]
-        across(lambda to: ch.at[s, to], m_in.at[s], 7 * s)
-        m_in[s, bank] = ch[s, bank]
+                ch[s, :, :, d, h] = chance[d * units : (d + 1) * units].reshape(nb // 2, 2, half, lanes)
+        remote(ch.at[s, :, 1 - side], near.at[s], 8 + nl * s, (bank ^ 1, lane))
         for h in range(2):
             for i, x in enumerate((re[h], im[h])):
                 out[i, :, :, h, s * half : (s + 1) * half] = x.reshape(depth, units, half, lanes)
 
     for s in range(2):
-        arrived(m_in.at[s], nb, recv, 7 * s)
+        pltpu.make_async_copy(near.at[s], near.at[s], recv.at[8 + nl * s]).wait()
+        pair[s] = ch[s, :, side] + near[s]
+
+        def one(to, carry):
+            @pl.when(to != pairs_at)
+            def _():
+                remote(pair.at[s, to], m_in.at[s, pairs_at], 7 * s, (2 * to + side, lane))
+
+            return carry
+
+        lax.fori_loop(0, nb // 2, one, 0)
+        m_in[s, pairs_at] = pair[s, pairs_at]
+    for s in range(2):
+        arrived(m_in.at[s], nb // 2, recv, 7 * s)
         total = m_in[s, 0]
-        for g in range(1, nb):
+        for g in range(1, nb // 2):
             total = total + m_in[s, g]
         marg[:, :, s * half : (s + 1) * half] = total * (1.0 / nb)
     for k in range(1, nl):
@@ -652,7 +662,8 @@
     for h in range(2):
         arrived(b_b.at[h], n, send, 2 + h)
         arrived(r_b.at[h], n, send, 5 + h)
-        arrived(m_in.at[h], nb, send, 7 * h)
+        arrived(m_in.at[h], nb // 2, send, 7 * h)
+        pltpu.make_async_copy(near.at[h], near.at[h], send.at[8 + nl * h]).wait()
     arrived(r_a, n, send, 4)
 
 
@@ -698,11 +709,13 @@
             level,
             level,
             pltpu.VMEM((2, 2, n, half, lanes), f32),
-            pltpu.VMEM((2, nb, depth, 2, half, lanes), f32),
-            pltpu.VMEM((2, nb, depth, 2, half, lanes), f32),
+            pltpu.VMEM((2, nb // 2, 2, depth, 2, half, lanes), f32),
+            pltpu.VMEM((2, nb // 2, depth, 2, half, lanes), f32),
+            pltpu.VMEM((2, nb // 2, depth, 2, half, lanes), f32),
+            pltpu.VMEM((2, nb // 2, depth, 2, half, lanes), f32),
             pltpu.SemaphoreType.DMA((4,)),
-            pltpu.SemaphoreType.DMA((8 + nl,)),
-            pltpu.SemaphoreType.DMA((8 + nl,)),
+            pltpu.SemaphoreType.DMA((9 + nl,)),
+            pltpu.SemaphoreType.DMA((9 + nl,)),
             *[pltpu.SemaphoreType.REGULAR] * 4,
         ],
         compiler_params=pltpu.CompilerParams(collective_id=0, has_side_effects=True),

time: 39.5 us -> 39.1 us (0.990)
  no operation moved by 1% of the time
where the time goes in v4:
time: 39.1 us; the launch traced here: 38.9 us
  Pallas kernels  38.3 us (98%)
  between operations  0.64 us (2%)
    pallas_call x1, Pallas kernels, in_pieces(): pl.pallas_call(functools.partial(pieces, nb, nl), name='register', out_sh...  37.5 us
    pallas_call x1, Pallas kernels, in_pieces(): pl.pallas_call(keep, name='keep', out_shape=tuple((jax.ShapeDtypeStruct(s...  0.81 us

profile of v4, /device:TPU:9, one launch (start us, length us, event | category | flops | bytes accessed | tf_op | source)
XLA Modules:
  0.0 38.9 jit_solution(14449109041514634340)
XLA Ops:
  0.6 37.5 %register.1 = (f32[2,4,8,2,8,128]{5,4,3,2,1,0:T(8,128)S(1)}, f32[4,2,8,128]{3,2,1,0:T(8,128)S(1)}) custom-call(f32[2,4,128,128]{3,2,1,0:T(8,128)} %amp_hbm.1, f32[8,4,16,128]{3,2,1,0:T(8,128)} %bitcast.3, f32[2,128]{1,0:T(2,128)} %ph_hbm.1, f32[2,4]{1,0:T(2,128)} %mix_hbm.1), custom_call_target="tpu_custom_call" | custom-call | tf_op jit(solution)/shard_map/register/pallas_call | solution.py:690
  38.1 0.8 %keep.1 = (f32[2,4,8,2,8,128]{5,4,3,2,1,0:T(8,128)}, f32[4,2,8,128]{3,2,1,0:T(8,128)}) custom-call(f32[2,4,8,2,8,128]{5,4,3,2,1,0:T(8,128)S(1)} %get-tuple-element.6.a, f32[4,2,8,128]{3,2,1,0:T(8,128)S(1)} %get-tuple-element.7.b), custom_call_target="tpu_custom_call" | custom-call | tf_op jit(solution)/shard_map/keep/pallas_call | solution.py:723

commit v5 on v4

--- a/solution.py
+++ b/solution.py
@@ -430,7 +430,7 @@
 
 def pieces(
     nb, nl, amp_hbm, en_hbm, ph_hbm, mix_hbm, out, marg,
-    ph, mix, amp, en, e_l, s_a, e_b, b_b, o_a, o_b, r_a, r_b, cs_b, sn_b, part, ch, near, pair, m_in,
+    ph, mix, turns, amp, en, e_l, s_a, e_b, b_b, o_a, o_b, r_a, r_b, cs_b, sn_b, part, ch, near, pair, m_in,
     load, send, recv, *met,
 ):
     n = nb * nl
@@ -475,15 +475,18 @@
     def now(to):
         return jnp.logical_or(lane != 2, to != 1)
 
+    other = jnp.where(lane < nl // 2, nl // 2, 0)
+    role = {"a": other, "b": other + 1, "t": lane ^ 1, "p": lane}
+
     def exchange(src, dst, which, order):
         for to in order:
-            send_lane(to, src, dst, which)
+            send_lane(role.get(to, to), src, dst, which)
         dst[me] = src[me]
 
     def along_line(k, start):
         to = lane ^ (nl - k)
         copy = pltpu.make_async_remote_copy(
-            src_ref=en.at[:, to],
+            src_ref=en_hbm.at[:, to],
             dst_ref=e_l.at[lane if start else to],
             send_sem=send.at[8 + k],
             recv_sem=recv.at[8 + k],
@@ -511,7 +514,7 @@
         pltpu.make_async_copy(most, most, sems.at[which]).wait()
 
     def angle(layer, group):
-        return cosines[layer : layer + 1, group : group + 1], sines[layer : layer + 1, group : group + 1]
+        return tuple(turns[i, layer : layer + 1, group : group + 1] for i in range(2))
 
     def mixed(layer, re, im, stride, stop, group):
         cosine, sine = (jnp.broadcast_to(x, re.shape[1:])[None, None] for x in angle(layer, group))
@@ -528,38 +531,41 @@
         real, imag = turn_table(count, *angle(layer, 1), places)
         return split(jnp.concatenate([jnp.concatenate([real, -imag], 1), jnp.concatenate([imag, real], 1)], 0))
 
-    loads[0].wait()
+    def prepare():
+        loads[0].wait()
+        loads[1].wait()
+        turns[0] = jnp.cos(mix[...])
+        turns[1] = jnp.sin(mix[...])
+        lane_first, row_first = lane_table(0), row_table(0, rows)
+        loads[2].wait()
+        loads[3].wait()
+
+        pairs = []
+        for d in range(depth):
+            e = en[pl.ds(d * units // nl, units // nl)].reshape(rows, lanes)
+            sine, cosine = sin_cos(ph[0:1] * e)
+            pairs.append((amp[0, d] * cosine + amp[1, d] * sine, amp[1, d] * cosine - amp[0, d] * sine))
+        re = jnp.stack([p[0] for p in pairs]).reshape(depth, rows // 8, 8, lanes)
+        im = jnp.stack([p[1] for p in pairs]).reshape(depth, rows // 8, 8, lanes)
+        cosine, sine = (jnp.broadcast_to(x, (8, lanes))[None] for x in angle(0, 2))
+        stride = 1
+        while stride < depth:
+            re, im = butterfly(re, im, stride, cosine, sine)
+            stride *= 2
+        re, im = re.reshape(depth, rows, lanes), im.reshape(depth, rows, lanes)
+        for d in range(depth):
+            both = dot3(split(jnp.concatenate([re[d], im[d]], 1)), lane_first)
+            both = dot3(row_first, split(jnp.concatenate([both[:, :lanes], both[:, lanes:]], 0)))
+            for i in range(2):
+                x = both[i * rows : (i + 1) * rows].reshape(units, 2, step, lanes)
+                for h in range(2):
+                    s_a[h, pl.ds(d * units, units), i] = x[:, h]
+
+    pl.when(lane == 0)(prepare)
     line()
     for k in range(1, nl):
         pl.when(known(lane ^ (nl - k)))(functools.partial(along_line, k, True))
-    loads[1].wait()
-    cosines, sines = jnp.cos(mix[...]), jnp.sin(mix[...])
-    lane_first, row_first = lane_table(0), row_table(0, rows)
-    lane_second, row_second = lane_table(1), row_table(1, lanes, step.bit_length() - 1)
-    loads[2].wait()
-    loads[3].wait()
-
-    pairs = []
-    for d in range(depth):
-        e = en[pl.ds(d * units // nl, units // nl)].reshape(rows, lanes)
-        sine, cosine = sin_cos(ph[0:1] * e)
-        pairs.append((amp[0, d] * cosine + amp[1, d] * sine, amp[1, d] * cosine - amp[0, d] * sine))
-    re = jnp.stack([p[0] for p in pairs]).reshape(depth, rows // 8, 8, lanes)
-    im = jnp.stack([p[1] for p in pairs]).reshape(depth, rows // 8, 8, lanes)
-    cosine, sine = (jnp.broadcast_to(x, (8, lanes))[None] for x in angle(0, 2))
-    stride = 1
-    while stride < depth:
-        re, im = butterfly(re, im, stride, cosine, sine)
-        stride *= 2
-    re, im = re.reshape(depth, rows, lanes), im.reshape(depth, rows, lanes)
-    for d in range(depth):
-        both = dot3(split(jnp.concatenate([re[d], im[d]], 1)), lane_first)
-        both = dot3(row_first, split(jnp.concatenate([both[:, :lanes], both[:, lanes:]], 0)))
-        for i in range(2):
-            x = both[i * rows : (i + 1) * rows].reshape(units, 2, step, lanes)
-            for h in range(2):
-                s_a[h, pl.ds(d * units, units), i] = x[:, h]
-
+    pl.when(lane != 0)(prepare)
     all_of_line()
     for k in range(1, nl):
         pl.when(jnp.logical_not(known(lane ^ (nl - k))))(functools.partial(along_line, k, True))
@@ -567,6 +573,7 @@
     across(lambda to: en.at[to, lane], e_b.at[:, lane], 1)
     e_b[bank, lane] = en[bank, lane]
     exchange(s_a.at[0], b_b.at[0], 2, (1, 2, 0, 3))
+    lane_second, row_second = lane_table(1), row_table(1, lanes, step.bit_length() - 1)
     for k in range(1, nl):
         source = along_line(k, False)
         across(lambda to: e_l.at[source, to], e_b.at[:, source], 1)
@@ -601,11 +608,11 @@
                 for s in range(2):
                     o_b[s, :, i] = x[:, s * half : (s + 1) * half]
         if h == 0:
-            for to in [0,2,1,3]:
+            for to in [role.get(x, x) for x in 'abtp']:
                 pl.when(now(to))(functools.partial(send_lane, to, o_a, r_a, 4))
             r_a[me] = o_a[me]
         else:
-            for to, s in [(0,0),(2,0),(0,1),(2,1),(1,-1),(1,0),(3,0),(1,1),(3,1)]:
+            for to, s in [(role.get(x, x), s) for x, s in [('a', 0), ('p', 0), ('a', 1), ('b', -1), ('p', 1), ('b', 0), ('t', 0), ('b', 1), ('t', 1)]]:
                 if s < 0:
                     pl.when(jnp.logical_not(now(to)))(functools.partial(send_lane, to, o_a, r_a, 4))
                 else:
@@ -696,6 +703,7 @@
         scratch_shapes=[
             pltpu.VMEM(phase_angles.shape, f32),
             pltpu.VMEM(mix_angles.shape, f32),
+            pltpu.VMEM((2, *mix_angles.shape), f32),
             pltpu.VMEM((2, depth, rows, lanes), f32),
             spread,
             pltpu.VMEM((nl, nb, per, lanes), f32),

time: 39.1 us -> 38.9 us (level)
  no operation moved by 1% of the time
where the time goes in v5:
time: 38.9 us; the launch traced here: 38.8 us
  Pallas kernels  38.1 us (98%)
  between operations  0.64 us (2%)
    pallas_call x1, Pallas kernels, in_pieces(): pl.pallas_call(functools.partial(pieces, nb, nl), name='register', out_sh...  37.3 us
    pallas_call x1, Pallas kernels, in_pieces(): pl.pallas_call(keep, name='keep', out_shape=tuple((jax.ShapeDtypeStruct(s...  0.81 us

profile of v5, /device:TPU:9, one launch (start us, length us, event | category | flops | bytes accessed | tf_op | source)
XLA Modules:
  0.0 38.8 jit_solution(15576057307102809609)
XLA Ops:
  0.6 37.3 %register.1 = (f32[2,4,8,2,8,128]{5,4,3,2,1,0:T(8,128)S(1)}, f32[4,2,8,128]{3,2,1,0:T(8,128)S(1)}) custom-call(f32[2,4,128,128]{3,2,1,0:T(8,128)} %amp_hbm.1, f32[8,4,16,128]{3,2,1,0:T(8,128)} %bitcast.3, f32[2,128]{1,0:T(2,128)} %ph_hbm.1, f32[2,4]{1,0:T(2,128)} %mix_hbm.1), custom_call_target="tpu_custom_call" | custom-call | tf_op jit(solution)/shard_map/register/pallas_call | solution.py:697
  38.0 0.8 %keep.1 = (f32[2,4,8,2,8,128]{5,4,3,2,1,0:T(8,128)}, f32[4,2,8,128]{3,2,1,0:T(8,128)}) custom-call(f32[2,4,8,2,8,128]{5,4,3,2,1,0:T(8,128)S(1)} %get-tuple-element.6.a, f32[4,2,8,128]{3,2,1,0:T(8,128)S(1)} %get-tuple-element.7.b), custom_call_target="tpu_custom_call" | custom-call | tf_op jit(solution)/shard_map/keep/pallas_call | solution.py:731

commit v6 on v5

--- a/solution.py
+++ b/solution.py
@@ -476,7 +476,8 @@
         return jnp.logical_or(lane != 2, to != 1)
 
     other = jnp.where(lane < nl // 2, nl // 2, 0)
-    role = {"a": other, "b": other + 1, "t": lane ^ 1, "p": lane}
+    early = jnp.where(lane == 1, 0, 1)
+    role = {"g": other + 1 - early, "h": other + early, "a": other, "b": other + 1, "t": lane ^ 1, "p": lane}
 
     def exchange(src, dst, which, order):
         for to in order:
@@ -612,8 +613,8 @@
                 pl.when(now(to))(functools.partial(send_lane, to, o_a, r_a, 4))
             r_a[me] = o_a[me]
         else:
-            for to, s in [(role.get(x, x), s) for x, s in [('a', 0), ('p', 0), ('a', 1), ('b', -1), ('p', 1), ('b', 0), ('t', 0), ('b', 1), ('t', 1)]]:
-                if s < 0:
+            for to, s in [(role.get(x, x), s) for x, s in [('a', 0), ('p', 0), ('g', early), ('b', -1), ('p', 1), ('h', 1 - early), ('t', 0), ('b', 1), ('t', 1)]]:
+                if isinstance(s, int) and s < 0:
                     pl.when(jnp.logical_not(now(to)))(functools.partial(send_lane, to, o_a, r_a, 4))
                 else:
                     send_lane(to, o_b.at[s], r_b.at[s], 5 + s)
@@ -648,14 +649,9 @@
         pltpu.make_async_copy(near.at[s], near.at[s], recv.at[8 + nl * s]).wait()
         pair[s] = ch[s, :, side] + near[s]
 
-        def one(to, carry):
-            @pl.when(to != pairs_at)
-            def _():
-                remote(pair.at[s, to], m_in.at[s, pairs_at], 7 * s, (2 * to + side, lane))
-
-            return carry
-
-        lax.fori_loop(0, nb // 2, one, 0)
+        for apart in range(nb // 2 - 1, 0, -1):
+            to = pairs_at ^ apart
+            remote(pair.at[s, to], m_in.at[s, pairs_at], 7 * s, (2 * to + side, lane))
         m_in[s, pairs_at] = pair[s, pairs_at]
     for s in range(2):
         arrived(m_in.at[s], nb // 2, recv, 7 * s)

time: 38.9 us -> 38.9 us (level)
  no operation moved by 1% of the time
where the time goes in v6:
time: 38.9 us; the launch traced here: 38.8 us
  Pallas kernels  38.2 us (98%)
  between operations  0.64 us (2%)
    pallas_call x1, Pallas kernels, in_pieces(): pl.pallas_call(functools.partial(pieces, nb, nl), name='register', out_sh...  37.3 us
    pallas_call x1, Pallas kernels, in_pieces(): pl.pallas_call(keep, name='keep', out_shape=tuple((jax.ShapeDtypeStruct(s...  0.81 us

profile of v6, /device:TPU:9, one launch (start us, length us, event | category | flops | bytes accessed | tf_op | source)
XLA Modules:
  0.0 38.8 jit_solution(2718782714338621223)
XLA Ops:
  0.6 37.3 %register.1 = (f32[2,4,8,2,8,128]{5,4,3,2,1,0:T(8,128)S(1)}, f32[4,2,8,128]{3,2,1,0:T(8,128)S(1)}) custom-call(f32[2,4,128,128]{3,2,1,0:T(8,128)} %amp_hbm.1, f32[8,4,16,128]{3,2,1,0:T(8,128)} %bitcast.3, f32[2,128]{1,0:T(2,128)} %ph_hbm.1, f32[2,4]{1,0:T(2,128)} %mix_hbm.1), custom_call_target="tpu_custom_call" | custom-call | tf_op jit(solution)/shard_map/register/pallas_call | solution.py:693
  38.0 0.8 %keep.1 = (f32[2,4,8,2,8,128]{5,4,3,2,1,0:T(8,128)}, f32[4,2,8,128]{3,2,1,0:T(8,128)}) custom-call(f32[2,4,8,2,8,128]{5,4,3,2,1,0:T(8,128)S(1)} %get-tuple-element.6.a, f32[4,2,8,128]{3,2,1,0:T(8,128)S(1)} %get-tuple-element.7.b), custom_call_target="tpu_custom_call" | custom-call | tf_op jit(solution)/shard_map/keep/pallas_call | solution.py:727

commit v7 on v5

--- a/solution.py
+++ b/solution.py
@@ -572,13 +572,13 @@
     everyone()
     across(lambda to: en.at[to, lane], e_b.at[:, lane], 1)
     e_b[bank, lane] = en[bank, lane]
-    exchange(s_a.at[0], b_b.at[0], 2, (1, 2, 0, 3))
+    exchange(s_a.at[0], b_b.at[0], 2, (1, 2, 3, 0))
     lane_second, row_second = lane_table(1), row_table(1, lanes, step.bit_length() - 1)
     for k in range(1, nl):
         source = along_line(k, False)
         across(lambda to: e_l.at[source, to], e_b.at[:, source], 1)
         e_b[bank, source] = e_l[source, bank]
-    exchange(s_a.at[1], b_b.at[1], 3, (1, 2, 0, 3))
+    exchange(s_a.at[1], b_b.at[1], 3, (1, 2, 3, 0))
     arrived(e_b, nb, recv, 1)
     sine, cosine = sin_cos(ph[1:2][None] * e_b[...].reshape(n, 2 * step, lanes))
     sn_b[...] = sine

time: 38.9 us -> 38.9 us (level)
  no operation moved by 1% of the time
where the time goes in v7:
time: 38.9 us; the launch traced here: 38.8 us
  Pallas kernels  38.2 us (98%)
  between operations  0.64 us (2%)
    pallas_call x1, Pallas kernels, in_pieces(): pl.pallas_call(functools.partial(pieces, nb, nl), name='register', out_sh...  37.3 us
    pallas_call x1, Pallas kernels, in_pieces(): pl.pallas_call(keep, name='keep', out_shape=tuple((jax.ShapeDtypeStruct(s...  0.81 us

profile of v7, /device:TPU:9, one launch (start us, length us, event | category | flops | bytes accessed | tf_op | source)
XLA Modules:
  0.0 38.8 jit_solution(15684067830347011855)
XLA Ops:
  0.6 37.3 %register.1 = (f32[2,4,8,2,8,128]{5,4,3,2,1,0:T(8,128)S(1)}, f32[4,2,8,128]{3,2,1,0:T(8,128)S(1)}) custom-call(f32[2,4,128,128]{3,2,1,0:T(8,128)} %amp_hbm.1, f32[8,4,16,128]{3,2,1,0:T(8,128)} %bitcast.3, f32[2,128]{1,0:T(2,128)} %ph_hbm.1, f32[2,4]{1,0:T(2,128)} %mix_hbm.1), custom_call_target="tpu_custom_call" | custom-call | tf_op jit(solution)/shard_map/register/pallas_call | solution.py:697
  38.0 0.8 %keep.1 = (f32[2,4,8,2,8,128]{5,4,3,2,1,0:T(8,128)}, f32[4,2,8,128]{3,2,1,0:T(8,128)}) custom-call(f32[2,4,8,2,8,128]{5,4,3,2,1,0:T(8,128)S(1)} %get-tuple-element.6.a, f32[4,2,8,128]{3,2,1,0:T(8,128)S(1)} %get-tuple-element.7.b), custom_call_target="tpu_custom_call" | custom-call | tf_op jit(solution)/shard_map/keep/pallas_call | solution.py:731
